TPU v7x, 32 devices: a whole 2x2x4 slice. The times are simulated.
32 devices in a mesh: face: 4 (over x, core), sub: 8 (over z, y).
Axes of the slice: x: 2, y: 2, z: 4, core: 2. Of those that a mesh axis runs over, the one named last changes fastest.
Arguments:
- grid_latent: bfloat16 [16384, 512], P(('face', 'sub')), may hold values from -6 to 6
- mesh_latent: bfloat16 [4096, 512], P(('face', 'sub')), may hold values from -6 to 6
- edge_latent: bfloat16 [32768, 512], P(('face', 'sub')), may hold values from -6 to 6
- mesh_cotangent: bfloat16 [4096, 512], P(('face', 'sub')), may hold values from -6 to 6
- edge_cotangent: bfloat16 [32768, 512], P(('face', 'sub')), may hold values from -6 to 6
- grid_send: int32 [32, 4, 256], P(('face', 'sub')), may hold values from 0 to 511
- grid_slot: int32 [32768], P(('face', 'sub')), may hold values from 0 to 1535, as said below
- grid_target: int32 [32768], P(('face', 'sub')), may hold values from 0 to 127
- mesh_halo: int32 [32, 4, 64], P(('face', 'sub')), may hold values from 0 to 127
- mesh_send: int32 [32, 32, 4], P(('face', 'sub')), may hold values from 0 to 127
- mesh_slot: int32 [32768], P(('face', 'sub')), may hold values from 0 to 511, as said below
- mesh_target: int32 [32768], P(('face', 'sub')), may hold values from 0 to 127
- weights: bfloat16 [10, 512, 512], replicated, may hold values from -0.25 to 0.25
Outputs:
- mesh_update: bfloat16 [4096, 512], P(('face', 'sub'))
- grid_grad: bfloat16 [16384, 512], P(('face', 'sub'))
- mesh_grad: bfloat16 [4096, 512], P(('face', 'sub'))
- edge_grad: bfloat16 [32768, 512], P(('face', 'sub'))
- weight_grads: bfloat16 [10, 512, 512], replicated
Inputs may be any that keep to these rules, and one draw needn't show every extreme that they name: grid_slot[e] names the edge device's own 512 grid rows or, above them, the 256 rows listed by each of its four neighbours in direction order. grid_target[e] is local to the edge's device. grid_send[q, k] lists local rows of device q for the device d with nb(d, k) = q; a row may appear in several slots. mesh_slot[e] names the own 128 mesh rows, then the 64 rows listed by each of the four neighbours, then 4 far rows from each device, source major. mesh_target[e] is local to the edge's device. mesh_halo[q, k] lists local rows of device q for its neighbour in direction k. mesh_send[q, d] lists local rows of device q for far edges of device d.
All inputs are finite; a program needn't handle non-finite values.
Results may differ from a plain program's by a relative error of at most 0.016.
Values may be sent and summed in bfloat16 or wider, within the bound.
A program may use at most 128 MiB of HBM per device.

v0:
```python
import jax
import jax.numpy as jnp
from jax import lax
from jax.sharding import PartitionSpec as P

norm_eps = 1e-05


def shifted(value, axis, steps):
    count = lax.axis_size(axis)
    pairs = [(source, (source + steps) % count) for source in range(count)]
    return lax.ppermute(value, axis, pairs)


def layer_norm(values):
    centre = values - jnp.mean(values, axis=-1, keepdims=True)
    spread = jnp.mean(centre * centre, axis=-1, keepdims=True)
    return centre * lax.rsqrt(spread + norm_eps)


def layer_norm_back(values, upstream):
    centre = values - jnp.mean(values, axis=-1, keepdims=True)
    inverse = lax.rsqrt(jnp.mean(centre * centre, axis=-1, keepdims=True) + norm_eps)
    normed = centre * inverse
    return inverse * (
        upstream
        - jnp.mean(upstream, axis=-1, keepdims=True)
        - normed * jnp.mean(upstream * normed, axis=-1, keepdims=True)
    )


def swish_slope(values):
    sigmoid_values = jax.nn.sigmoid(values)
    return sigmoid_values * (1.0 + values * (1.0 - sigmoid_values))


def product(former, latter):
    return jnp.dot(former, latter, preferred_element_type=jnp.float32)


def outer_sum(former, latter):
    return lax.dot_general(
        former, latter, (((0,), (0,)), ((), ())), preferred_element_type=jnp.float32
    )


def back_product(former, latter):
    return lax.dot_general(
        former, latter, (((1,), (1,)), ((), ())), preferred_element_type=jnp.float32
    )


def receive_sum(onehot, values):
    upper = values.astype(jnp.bfloat16)
    lower = (values - upper.astype(jnp.float32)).astype(jnp.bfloat16)
    return outer_sum(onehot, upper) + outer_sum(onehot, lower)


def grid_neighbours(outgoing):
    from_sub = [shifted(outgoing[block], "sub", offset) for block, offset in ((0, 1), (1, -1))]
    from_face = [shifted(outgoing[block], "face", offset) for block, offset in ((2, 1), (3, -1))]
    return jnp.concatenate(from_sub + from_face, axis=0)


def grid_returns(partials):
    to_sub = [shifted(partials[block], "sub", offset) for block, offset in ((0, -1), (1, 1))]
    to_face = [shifted(partials[block], "face", offset) for block, offset in ((2, -1), (3, 1))]
    return jnp.concatenate(to_sub + to_face, axis=0)


def mesh_neighbours(outgoing):
    from_sub = [shifted(outgoing[block], "sub", offset) for block, offset in ((0, 1), (1, -1))]
    from_face = [shifted(outgoing[block], "face", offset) for block, offset in ((2, 1), (3, -1))]
    return jnp.concatenate(from_sub + from_face, axis=0)


def mesh_returns(partials):
    to_sub = [shifted(partials[block], "sub", offset) for block, offset in ((0, -1), (1, 1))]
    to_face = [shifted(partials[block], "face", offset) for block, offset in ((2, -1), (3, 1))]
    return jnp.concatenate(to_sub + to_face, axis=0)


def move_mesh(outgoing):
    return lax.all_to_all(outgoing, ("face", "sub"), split_axis=0, concat_axis=0, tiled=True)


def return_mesh(outgoing):
    return lax.all_to_all(outgoing, ("face", "sub"), split_axis=0, concat_axis=0, tiled=True)


def on_device(
    grid_latent,
    mesh_latent,
    edge_latent,
    mesh_cotangent,
    edge_cotangent,
    grid_send,
    grid_slot,
    grid_target,
    mesh_halo,
    mesh_send,
    mesh_slot,
    mesh_target,
    weights,
):
    peer_count = lax.axis_size("face") * lax.axis_size("sub")
    latent = weights.shape[1]
    mesh_rows = mesh_latent.shape[0]
    grid_rows = grid_latent.shape[0]
    grid_table = grid_send[0].reshape(-1)
    halo_table = mesh_halo[0].reshape(-1)
    far_table = mesh_send[0].reshape(-1)
    halo_count = halo_table.shape[0]
    node_ids = jnp.arange(mesh_rows, dtype=jnp.int32)
    grid_project = product(grid_latent, weights[0]).astype(jnp.bfloat16)
    grid_outgoing = jnp.take(grid_project, grid_table, axis=0).reshape(4, -1, latent)
    grid_source = jnp.concatenate([grid_project, grid_neighbours(grid_outgoing)], axis=0)
    encode_receive = product(mesh_latent, weights[1])
    encoder_pre = jnp.take(grid_source, grid_slot, axis=0).astype(jnp.float32) + jnp.take(
        encode_receive, grid_target, axis=0
    )
    encoder_hidden = jax.nn.silu(encoder_pre).astype(jnp.bfloat16)
    encoder_linear = product(encoder_hidden, weights[2])
    encoder_message = layer_norm(encoder_linear).astype(jnp.bfloat16)
    grid_onehot = (grid_target[:, None] == node_ids[None, :]).astype(jnp.bfloat16)
    encoder_total = outer_sum(grid_onehot, encoder_message)
    mesh_middle = (mesh_latent.astype(jnp.float32) + encoder_total).astype(jnp.bfloat16)
    sender_rows = product(mesh_middle, weights[4]).astype(jnp.bfloat16)
    halo_outgoing = jnp.take(sender_rows, halo_table, axis=0).reshape(4, -1, latent)
    far_outgoing = jnp.take(sender_rows, far_table, axis=0).reshape(peer_count, -1, latent)
    far_incoming = move_mesh(far_outgoing).reshape(-1, latent)
    mesh_source = jnp.concatenate(
        [sender_rows, mesh_neighbours(halo_outgoing), far_incoming], axis=0
    )
    process_receive = product(mesh_middle, weights[5])
    process_pre = (
        product(edge_latent, weights[3])
        + jnp.take(mesh_source, mesh_slot, axis=0).astype(jnp.float32)
        + jnp.take(process_receive, mesh_target, axis=0)
    )
    process_hidden = jax.nn.silu(process_pre).astype(jnp.bfloat16)
    process_linear = product(process_hidden, weights[6])
    edge_update = layer_norm(process_linear).astype(jnp.bfloat16)
    mesh_onehot = (mesh_target[:, None] == node_ids[None, :]).astype(jnp.bfloat16)
    process_round = outer_sum(mesh_onehot, edge_update).astype(jnp.bfloat16)
    update_pre = product(mesh_middle, weights[7]) + product(process_round, weights[8])
    update_hidden = jax.nn.silu(update_pre).astype(jnp.bfloat16)
    update_linear = product(update_hidden, weights[9])
    mesh_update = (mesh_middle.astype(jnp.float32) + layer_norm(update_linear)).astype(jnp.bfloat16)
    outer_cot = mesh_cotangent.astype(jnp.float32)
    cot_linear = layer_norm_back(update_linear, outer_cot).astype(jnp.bfloat16)
    grad_update_output = outer_sum(update_hidden, cot_linear)
    cot_update = (back_product(cot_linear, weights[9]) * swish_slope(update_pre)).astype(
        jnp.bfloat16
    )
    grad_update_self = outer_sum(mesh_middle, cot_update)
    grad_update_message = outer_sum(process_round, cot_update)
    cot_total = back_product(cot_update, weights[8])
    edge_cot = edge_cotangent.astype(jnp.float32)
    cot_edge = jnp.take(cot_total, mesh_target, axis=0) + edge_cot
    cot_plinear = layer_norm_back(process_linear, cot_edge).astype(jnp.bfloat16)
    grad_process_output = outer_sum(process_hidden, cot_plinear)
    cot_process = back_product(cot_plinear, weights[6]) * swish_slope(process_pre)
    cot_round = cot_process.astype(jnp.bfloat16)
    grad_process_edge = outer_sum(edge_latent, cot_round)
    edge_grad = (edge_cot + back_product(cot_round, weights[3])).astype(jnp.bfloat16)
    cot_receive = receive_sum(mesh_onehot, cot_process).astype(jnp.bfloat16)
    grad_process_receiver = outer_sum(mesh_middle, cot_receive)
    cot_slot = jax.ops.segment_sum(cot_process, mesh_slot, num_segments=mesh_source.shape[0])
    halo_partials = (
        cot_slot[mesh_rows : mesh_rows + halo_count].astype(jnp.bfloat16).reshape(4, -1, latent)
    )
    far_partials = (
        cot_slot[mesh_rows + halo_count :].astype(jnp.bfloat16).reshape(peer_count, -1, latent)
    )
    halo_returned = mesh_returns(halo_partials).astype(jnp.float32)
    far_returned = return_mesh(far_partials).reshape(-1, latent).astype(jnp.float32)
    sender_total = (
        cot_slot[:mesh_rows]
        + jax.ops.segment_sum(halo_returned, halo_table, num_segments=mesh_rows)
        + jax.ops.segment_sum(far_returned, far_table, num_segments=mesh_rows)
    )
    cot_sender = sender_total.astype(jnp.bfloat16)
    grad_process_sender = outer_sum(mesh_middle, cot_sender)
    cot_middle = (
        outer_cot
        + back_product(cot_update, weights[7])
        + back_product(cot_receive, weights[5])
        + back_product(cot_sender, weights[4])
    )
    process_grads = jnp.stack(
        [
            grad_process_edge,
            grad_process_sender,
            grad_process_receiver,
            grad_process_output,
            grad_update_self,
            grad_update_message,
            grad_update_output,
        ]
    )
    process_grads = lax.psum(process_grads, ("face", "sub"))
    cot_message = jnp.take(cot_middle, grid_target, axis=0)
    cot_elinear = layer_norm_back(encoder_linear, cot_message).astype(jnp.bfloat16)
    grad_encode_output = outer_sum(encoder_hidden, cot_elinear)
    cot_encoder = back_product(cot_elinear, weights[2]) * swish_slope(encoder_pre)
    cot_mesh_receive = receive_sum(grid_onehot, cot_encoder).astype(jnp.bfloat16)
    grad_encode_receiver = outer_sum(mesh_latent, cot_mesh_receive)
    mesh_grad = (cot_middle + back_product(cot_mesh_receive, weights[1])).astype(jnp.bfloat16)
    cot_gslot = jax.ops.segment_sum(cot_encoder, grid_slot, num_segments=grid_source.shape[0])
    grid_partials = cot_gslot[grid_rows:].astype(jnp.bfloat16).reshape(4, -1, latent)
    grid_returned = grid_returns(grid_partials).astype(jnp.float32)
    cot_grid = (
        cot_gslot[:grid_rows]
        + jax.ops.segment_sum(grid_returned, grid_table, num_segments=grid_rows)
    ).astype(jnp.bfloat16)
    grad_encode_sender = outer_sum(grid_latent, cot_grid)
    grid_grad = back_product(cot_grid, weights[0]).astype(jnp.bfloat16)
    encode_grads = jnp.stack([grad_encode_sender, grad_encode_receiver, grad_encode_output])
    encode_grads = lax.psum(encode_grads, ("face", "sub"))
    summed = jnp.concatenate([encode_grads, process_grads], axis=0)
    encode_scale = 1.0 / (grid_slot.shape[0] * peer_count) ** 0.5
    process_scale = 1.0 / (mesh_slot.shape[0] * peer_count) ** 0.5
    update_scale = 1.0 / (mesh_rows * peer_count) ** 0.5
    scale_column = jnp.array(
        [encode_scale] * 3 + [process_scale] * 4 + [update_scale] * 3, jnp.float32
    )
    weight_grads = (summed * scale_column[:, None, None]).astype(jnp.bfloat16)
    return (mesh_update, grid_grad, mesh_grad, edge_grad, weight_grads)


def solution(mesh):
    return jax.shard_map(
        on_device,
        mesh=mesh,
        in_specs=(
            P(("face", "sub"), None),
            P(("face", "sub"), None),
            P(("face", "sub"), None),
            P(("face", "sub"), None),
            P(("face", "sub"), None),
            P(("face", "sub"), None, None),
            P(("face", "sub")),
            P(("face", "sub")),
            P(("face", "sub"), None, None),
            P(("face", "sub"), None, None),
            P(("face", "sub")),
            P(("face", "sub")),
            P(),
        ),
        out_specs=(
            P(("face", "sub"), None),
            P(("face", "sub"), None),
            P(("face", "sub"), None),
            P(("face", "sub"), None),
            P(),
        ),
        check_vma=False,
    )
```

profile of v0, /device:TPU:0, one launch (start us, length us, event | category | flops | bytes accessed | tf_op | source)
XLA Modules:
  0.0 434.6 jit_solution(5734349062935372784)
XLA Ops:
  8.6 1.7 constant_dynamic-update-slice_fusion.4
  10.3 5.1 %gather_fusion.3 = bf16[1024,512]{1,0:T(8,128)(2,1)} fusion(bf16[512,512]{1,0:T(8,128)(2,1)S(1)} %get-tuple-element.43, s32[1024]{0:T(1024)S(1)} %fusion.116), kind=kCustom, calls=%fused_computation.clone | custom fusion | bytes 2101248 | tf_op jit(solution)/shard_map/jit(_take)/gather | solution.py:116
  15.4 1.5 broadcast_select_fusion
  17.9 2.4 collective-permute-start.3
  20.3 4.6 %collective-permute-start.1 = (bf16[256,512]{1,0:T(8,128)(2,1)}, bf16[256,512]{1,0:T(8,128)(2,1)}, u32[]{:S(2)}, u32[]{:S(2)}) collective-permute-start(bf16[256,512]{1,0:T(8,128)(2,1)} %get-tuple-element.31), channel_id=1, source_target_pairs={{0,7},{1,0},{2,1},{3,2},{4,3},{5,4},{6,5},{7,6},{8,15},{9,8},{10,9... | collective-permute-start | bytes 786440 | tf_op jit(solution)/shard_map/ppermute | solution.py:12
  31.7 1.3 pad_clamp_fusion
  34.5 2.3 copy.38
  36.7 4.9 %gather_fusion.4 = f32[1024,512]{1,0:T(8,128)} fusion(f32[128,512]{1,0:T(8,128)S(1)} %fusion.58, s32[1024]{0:T(1024)S(1)} %copy-done.50), kind=kCustom, calls=%fused_computation.1.clone | custom fusion | bytes 4198400 | tf_op jit(solution)/shard_map/jit(_take)/gather | solution.py:119
  43.7 5.1 %gather_fusion = bf16[1024,512]{1,0:T(8,128)(2,1)} fusion(bf16[1536,512]{1,0:T(8,128)(2,1)S(1)} %constant_dynamic-update-slice_fusion, s32[1024]{0:T(1024)S(1)} %copy-done.55), kind=kCustom, calls=%fused_computation.6 | custom fusion | bytes 2101248 | tf_op jit(solution)/shard_map/jit(_take)/gather | solution.py:119
  48.8 2.3 multiply_convert_fusion.3
  51.1 2.2 fusion.127
  55.9 2.0 fusion.52
  57.9 1.3 constant_dynamic-update-slice_fusion.10
  60.2 1.3 gather_fusion.1
  62.5 6.1 %all-to-all-start = ((bf16[32,4,512]{2,1,0:T(4,128)(2,1)}), bf16[32,4,512]{2,1,0:T(4,128)(2,1)S(1)}, u32[]{:S(2)}, u32[]{:S(2)}) async-start(bf16[32,4,512]{2,1,0:T(4,128)(2,1)} %broadcast_select_fusion.3), calls=%async_computation | async-start | bytes 262144 | tf_op jit(solution)/shard_map/all_to_all | solution.py:84
  68.7 1.5 collective-permute-start.7
  70.2 4.4 %collective-permute-start.5 = (bf16[64,512]{1,0:T(8,128)(2,1)S(1)}, bf16[64,512]{1,0:T(8,128)(2,1)S(1)}, u32[]{:S(2)}, u32[]{:S(2)}) collective-permute-start(bf16[64,512]{1,0:T(8,128)(2,1)S(1)} %get-tuple-element.40), channel_id=1, source_target_pairs={{0,7},{1,0},{2,1},{3,2},{4,3},{5,4},{6,5},{7,6},{8,15},{9,8},{10,9... | collective-permute-start | bytes 196616 | tf_op jit(solution)/shard_map/ppermute | solution.py:12
  74.6 4.9 %gather_fusion.6 = f32[1024,512]{1,0:T(8,128)} fusion(f32[128,512]{1,0:T(8,128)S(1)} %fusion.44, s32[1024]{0:T(1024)S(1)} %copy-done.52), kind=kCustom, calls=%fused_computation.3.clone | custom fusion | bytes 4198400 | tf_op jit(solution)/shard_map/jit(_take)/gather | solution.py:139
  79.7 4.0 gather_fusion.5
  83.7 4.1 multiply_convert_fusion.2
  87.9 2.2 fusion.128
  91.2 1.3 convolution_add_fusion.4
  92.6 1.5 fusion.129
  96.2 1.4 fusion.15
  97.6 1.4 fusion.37
  99.0 2.1 convolution_add_fusion.3
  101.1 5.1 %gather_fusion.7 = f32[1024,512]{1,0:T(8,128)} fusion(f32[128,512]{1,0:T(8,128)S(1)} %fusion.37, s32[1024]{0:T(1024)} %get-tuple-element.61), kind=kCustom, calls=%fused_computation.4.clone | custom fusion | bytes 4198400 | tf_op jit(solution)/shard_map/jit(_take)/gather | solution.py:160
  106.3 2.9 copy.37
  109.2 2.7 fusion.33
  114.9 4.0 fusion.130
  118.9 7.8 %scatter_custom_fusion = f32[512,512]{1,0:T(8,128)S(1)} fusion(s32[1024]{0:T(1024)} %param.28, f32[1024,512]{1,0:T(8,128)} %get-tuple-element.55, f32[]{:T(128)} %constant.90.clone.1), kind=kCustom, calls=%fused_computation.127 | custom fusion | flops 524288 | bytes 1049088 | tf_op jit(solution)/shard_map/scatter-add | solution.py:169
  128.3 1.8 fusion.14
  131.7 2.9 all-to-all-start.1
  134.7 4.8 %collective-permute-start.8 = (bf16[64,512]{1,0:T(8,128)(2,1)}, bf16[64,512]{1,0:T(8,128)(2,1)S(1)}, u32[]{:S(2)}, u32[]{:S(2)}) collective-permute-start(bf16[64,512]{1,0:T(8,128)(2,1)} %get-tuple-element.33), channel_id=1, source_target_pairs={{0,7},{1,0},{2,1},{3,2},{4,3},{5,4},{6,5},{7,6},{8,15},{9,8},{10,9... | collective-permute-start | bytes 196616 | tf_op jit(solution)/shard_map/ppermute | solution.py:12
  139.5 1.7 collective-permute-start.10
  141.3 1.4 convolution_add_fusion.2
  143.4 4.8 %collective-permute-done.9 = bf16[64,512]{1,0:T(8,128)(2,1)S(1)} collective-permute-done((bf16[64,512]{1,0:T(8,128)(2,1)S(1)}, bf16[64,512]{1,0:T(8,128)(2,1)S(1)}, u32[]{:S(2)}, u32[]{:S(2)}) %collective-permute-start.9) | collective-permute-done | bytes 65568 | tf_op jit(solution)/shard_map/ppermute | solution.py:12
  148.2 2.4 scatter_custom_fusion.1
  150.7 1.5 scatter_custom_fusion.2
  152.2 1.4 convolution_add_fusion.1
  153.6 4.9 %gather_fusion.8 = f32[1024,512]{1,0:T(8,128)} fusion(f32[128,512]{1,0:T(8,128)S(1)} %convolution_add_fusion.1, s32[1024]{0:T(1024)S(1)} %copy-done.51), kind=kCustom, calls=%fused_computation.5.clone | custom fusion | bytes 4198400 | tf_op jit(solution)/shard_map/jit(_take)/gather | solution.py:203
  158.5 3.1 copy.40
  161.6 2.3 select_reduce_fusion
  165.8 2.7 multiply_multiply_fusion
  168.5 1.7 convolution_bitcast_fusion.1
  170.8 8.5 %scatter_custom_fusion.3 = f32[1536,512]{1,0:T(8,128)} fusion(s32[1024]{0:T(1024)} %param.24, f32[1024,512]{1,0:T(8,128)S(1)} %multiply_multiply_fusion, f32[]{:T(128)} %constant.90.clone.1), kind=kCustom, calls=%fused_computation.43 | custom fusion | flops 524288 | bytes 3146240 | tf_op jit(solution)/shard_map/scatter-add | solution.py:210
  179.3 2.1 convert.9
  182.9 1.7 collective-permute-start.14
  184.6 2.2 collective-permute-start.13
  186.8 1.3 fusion.13
  188.1 1.3 fusion.12
  189.4 1.7 fusion.8
  191.2 1.3 fusion.11
  192.5 1.3 fusion.10
  193.9 1.5 fusion.9
  196.9 8.2 %scatter_custom_fusion.4 = f32[512,512]{1,0:T(8,128)S(1)} fusion(f32[512,512]{1,0:T(8,128)S(1)} %slice-done, s32[1024]{0:T(1024)} %bitcast.150, bf16[256,512]{1,0:T(8,128)(2,1)} %copy-done.36, bf16[]{:T(256)} %constant.108, bf16[256,512]{1,0:T(8,128)(2,1)} %copy-done.37, bf16[256,512]{1,0:T(8,128)(2,1)} %collective-permute-done.13, ...), kind=kCustom, calls=%fused_computation.23 | custom fusion | flops 4718592 | bytes 2097664 | tf_op jit(solution)/shard_map/scatter-add | solution.py:215
  205.6 3.2 pad_maximum_fusion
  210.0 3.1 fusion.1
  213.1 2.5 copy.49
  215.6 2.0 fusion.16
  217.7 2.3 convolution_convert_fusion
  220.0 191.5 %all-reduce.3.cloned.1.call-done = (f32[7,512,512]{1,2,0:T(8,128)}, f32[3,512,512]{1,2,0:T(8,128)}) async-done(((f32[7,512,512]{1,2,0:T(8,128)}, f32[3,512,512]{1,2,0:T(8,128)}), (f32[7,512,512]{1,2,0:T(8,128)}, f32[3,512,512]{1,2,0:T(8,128)})) %all-reduce.3.cloned.1.call-update) | async-done | bytes 10485776 | tf_op jit(solution)/shard_map/psum | solution.py:202
  411.4 7.9 %fusion = bf16[10,512,512]{1,2,0:T(8,128)(2,1)} fusion(f32[7,512,512]{1,2,0:T(8,128)} %get-tuple-element.23, f32[3,512,512]{1,2,0:T(8,128)} %get-tuple-element.24, f32[10]{0:T(128)S(1)} %copy-done.71), kind=kLoop, calls=%fused_computation.15 | loop fusion | flops 7864320 | bytes 15728680 | tf_op jit(solution)/shard_map/convert_element_type | solution.py:228
  419.3 8.0 %copy.50 = bf16[10,512,512]{2,1,0:T(8,128)(2,1)} copy(bf16[10,512,512]{1,2,0:T(8,128)(2,1)} %fusion) | data formatting | bytes 10485760
  (259 shorter events, 34.6 us)
Async XLA Ops:
  7.2 76.5 %copy-start = (bf16[1024,512]{1,0:T(8,128)(2,1)S(1)}, bf16[1024,512]{1,0:T(8,128)(2,1)}, u32[]{:S(2)}) copy-start(bf16[1024,512]{1,0:T(8,128)(2,1)} %param.20) | copy-start | bytes 3145732
  15.4 9.5 %copy-start.63 = (s32[1,4,64]{2,1,0:T(4,128)S(1)}, s32[1,4,64]{2,1,0:T(4,128)}, u32[]{:S(2)}) copy-start(s32[1,4,64]{2,1,0:T(4,128)} %param.26) | copy-start | bytes 3076
  15.4 9.7 %copy-start.40 = (s32[1024]{0:T(1024)S(1)}, s32[1024]{0:T(1024)}, u32[]{:S(2)}) copy-start(s32[1024]{0:T(1024)} %param.25) | copy-start | bytes 12292
  15.4 9.7 %copy-start.57 = (s32[1024]{0:T(1024)S(1)}, s32[1024]{0:T(1024)}, u32[]{:S(2)}) copy-start(s32[1024]{0:T(1024)} %param.24) | copy-start | bytes 12292
  15.4 10.9 %copy-start.42 = (s32[1024]{0:T(1024)S(1)}, s32[1024]{0:T(1024)}, u32[]{:S(2)}) copy-start(s32[1024]{0:T(1024)} %param.29) | copy-start | bytes 12292
  15.4 10.9 %copy-start.56 = (s32[1024]{0:T(1024)S(1)}, s32[1024]{0:T(1024)}, u32[]{:S(2)}) copy-start(s32[1024]{0:T(1024)} %param.28) | copy-start | bytes 12292
  15.4 12.0 %copy-start.62 = (s32[1,32,4]{1,2,0:T(4,128)S(1)}, s32[1,32,4]{1,2,0:T(4,128)}, u32[]{:S(2)}) copy-start(s32[1,32,4]{1,2,0:T(4,128)} %param.27) | copy-start | bytes 1540
  15.4 14.4 %copy-start.18 = (bf16[128,512]{1,0:T(8,128)(2,1)S(1)}, bf16[128,512]{1,0:T(8,128)(2,1)}, u32[]{:S(2)}) copy-start(bf16[128,512]{1,0:T(8,128)(2,1)} %param.19) | copy-start | bytes 393220
  17.9 25.7 %collective-permute-start.3 = (bf16[256,512]{1,0:T(8,128)(2,1)}, bf16[256,512]{1,0:T(8,128)(2,1)S(1)}, u32[]{:S(2)}, u32[]{:S(2)}) collective-permute-start(bf16[256,512]{1,0:T(8,128)(2,1)} %get-tuple-element.29), channel_id=1, source_target_pairs={{0,24},{8,0},{16,8},{24,16},{1,25},{9,1},{17,9},{25,17},{2,26},{10... | collective-permute-start | bytes 786440 | tf_op jit(solution)/shard_map/ppermute | solution.py:12
  20.3 23.3 %collective-permute-start.2 = (bf16[256,512]{1,0:T(8,128)(2,1)}, bf16[256,512]{1,0:T(8,128)(2,1)S(1)}, u32[]{:S(2)}, u32[]{:S(2)}) collective-permute-start(bf16[256,512]{1,0:T(8,128)(2,1)} %get-tuple-element.30), channel_id=1, source_target_pairs={{0,8},{8,16},{16,24},{24,0},{1,9},{9,17},{17,25},{25,1},{2,10},{10... | collective-permute-start | bytes 786440 | tf_op jit(solution)/shard_map/ppermute | solution.py:12
  20.3 22.3 %collective-permute-start.1 = (bf16[256,512]{1,0:T(8,128)(2,1)}, bf16[256,512]{1,0:T(8,128)(2,1)}, u32[]{:S(2)}, u32[]{:S(2)}) collective-permute-start(bf16[256,512]{1,0:T(8,128)(2,1)} %get-tuple-element.31), channel_id=1, source_target_pairs={{0,7},{1,0},{2,1},{3,2},{4,3},{5,4},{6,5},{7,6},{8,15},{9,8},{10,9... | collective-permute-start | bytes 786440 | tf_op jit(solution)/shard_map/ppermute | solution.py:12
  24.9 16.7 %collective-permute-start = (bf16[256,512]{1,0:T(8,128)(2,1)}, bf16[256,512]{1,0:T(8,128)(2,1)}, u32[]{:S(2)}, u32[]{:S(2)}) collective-permute-start(bf16[256,512]{1,0:T(8,128)(2,1)} %get-tuple-element.32), channel_id=1, source_target_pairs={{0,1},{1,2},{2,3},{3,4},{4,5},{5,6},{6,7},{7,0},{8,9},{9,10},{10,1... | collective-permute-start | bytes 786440 | tf_op jit(solution)/shard_map/ppermute | solution.py:12
  24.9 4.2 copy-start.68
  33.7 3.1 copy-start.50
  43.7 5.1 %copy-start.58 = (pred[1024]{0:T(1024)(128)(4,1)S(1)}, pred[1024]{0:T(1024)(128)(4,1)}, u32[]{:S(2)}) copy-start(pred[1024]{0:T(1024)(128)(4,1)} %get-tuple-element.62) | copy-start | bytes 3076
  43.7 5.1 %copy-start.64 = (pred[1024]{0:T(1024)(128)(4,1)S(1)}, pred[1024]{0:T(1024)(128)(4,1)}, u32[]{:S(2)}) copy-start(pred[1024]{0:T(1024)(128)(4,1)} %get-tuple-element.63) | copy-start | bytes 3076
  53.7 4.3 copy-start.46
  60.2 14.5 %copy-start.52 = (s32[1024]{0:T(1024)S(1)}, s32[1024]{0:T(1024)}, u32[]{:S(2)}) copy-start(s32[1024]{0:T(1024)} %get-tuple-element.61) | copy-start | bytes 12292
  61.7 17.9 %collective-permute-start.4 = (bf16[64,512]{1,0:T(8,128)(2,1)S(1)}, bf16[64,512]{1,0:T(8,128)(2,1)S(1)}, u32[]{:S(2)}, u32[]{:S(2)}) collective-permute-start(bf16[64,512]{1,0:T(8,128)(2,1)S(1)} %get-tuple-element.41), channel_id=1, source_target_pairs={{0,1},{1,2},{2,3},{3,4},{4,5},{5,6},{6,7},{7,0},{8,9},{9,10},{10,1... | collective-permute-start | bytes 196616 | tf_op jit(solution)/shard_map/ppermute | solution.py:12
  62.5 17.1 %all-to-all-start = ((bf16[32,4,512]{2,1,0:T(4,128)(2,1)}), bf16[32,4,512]{2,1,0:T(4,128)(2,1)S(1)}, u32[]{:S(2)}, u32[]{:S(2)}) async-start(bf16[32,4,512]{2,1,0:T(4,128)(2,1)} %broadcast_select_fusion.3), calls=%async_computation | async-start | bytes 262144 | tf_op jit(solution)/shard_map/all_to_all | solution.py:84
  68.7 10.9 %collective-permute-start.7 = (bf16[64,512]{1,0:T(8,128)(2,1)S(1)}, bf16[64,512]{1,0:T(8,128)(2,1)S(1)}, u32[]{:S(2)}, u32[]{:S(2)}) collective-permute-start(bf16[64,512]{1,0:T(8,128)(2,1)S(1)} %get-tuple-element.38), channel_id=1, source_target_pairs={{0,24},{8,0},{16,8},{24,16},{1,25},{9,1},{17,9},{25,17},{2,26},{10... | collective-permute-start | bytes 196616 | tf_op jit(solution)/shard_map/ppermute | solution.py:12
  70.2 9.4 %collective-permute-start.6 = (bf16[64,512]{1,0:T(8,128)(2,1)S(1)}, bf16[64,512]{1,0:T(8,128)(2,1)S(1)}, u32[]{:S(2)}, u32[]{:S(2)}) collective-permute-start(bf16[64,512]{1,0:T(8,128)(2,1)S(1)} %get-tuple-element.39), channel_id=1, source_target_pairs={{0,8},{8,16},{16,24},{24,0},{1,9},{9,17},{17,25},{25,1},{2,10},{10... | collective-permute-start | bytes 196616 | tf_op jit(solution)/shard_map/ppermute | solution.py:12
  70.2 9.3 %collective-permute-start.5 = (bf16[64,512]{1,0:T(8,128)(2,1)S(1)}, bf16[64,512]{1,0:T(8,128)(2,1)S(1)}, u32[]{:S(2)}, u32[]{:S(2)}) collective-permute-start(bf16[64,512]{1,0:T(8,128)(2,1)S(1)} %get-tuple-element.40), channel_id=1, source_target_pairs={{0,7},{1,0},{2,1},{3,2},{4,3},{5,4},{6,5},{7,6},{8,15},{9,8},{10,9... | collective-permute-start | bytes 196616 | tf_op jit(solution)/shard_map/ppermute | solution.py:12
  74.6 5.0 %copy-start.54 = (s32[1024]{0:T(1024)S(1)}, s32[1024]{0:T(1024)}, u32[]{:S(2)}) copy-start(s32[1024]{0:T(1024)} %get-tuple-element.60) | copy-start | bytes 12292
  79.7 4.0 copy-start.60
  79.7 4.0 copy-start.69
  83.7 4.2 copy-start.22
  90.4 3.6 copy-start.48
  91.2 3.9 copy-start.20
  91.2 3.1 copy-start.33
  92.6 5.1 %copy-start.38 = (f32[128,512]{1,0:T(8,128)}, f32[128,512]{1,0:T(8,128)S(1)}, u32[]{:S(2)}) copy-start(f32[128,512]{1,0:T(8,128)S(1)} %convolution_add_fusion.4) | copy-start | bytes 786436
  94.0 5.0 %copy-start.24 = (f32[128,512]{1,0:T(8,128)}, f32[128,512]{1,0:T(8,128)S(1)}, u32[]{:S(2)}) copy-start(f32[128,512]{1,0:T(8,128)S(1)} %get-tuple-element.53) | copy-start | bytes 786436
  106.2 2.9 copy-start.49
  106.2 2.9 copy-start.61
  109.2 2.8 copy-start.6
  112.0 2.9 copy-start.79
  112.7 6.2 %copy-start.29 = (bf16[1024,512]{0,1:T(8,128)(2,1)}, bf16[1024,512]{0,1:T(8,128)(2,1)S(1)}, u32[]{:S(2)}) copy-start(bf16[1024,512]{0,1:T(8,128)(2,1)S(1)} %multiply_convert_fusion.1) | copy-start | bytes 3145732
  118.9 11.1 %copy-start.10 = (bf16[1024,512]{1,0:T(8,128)(2,1)}, bf16[1024,512]{1,0:T(8,128)(2,1)S(1)}, u32[]{:S(2)}) copy-start(bf16[1024,512]{1,0:T(8,128)(2,1)S(1)} %get-tuple-element.54) | copy-start | bytes 3145732
  130.1 9.4 %copy-start.45 = (bf16[64,512]{1,0:T(8,128)(2,1)S(1)}, bf16[64,512]{1,0:T(8,128)(2,1)}, u32[]{:S(2)}) copy-start(bf16[64,512]{1,0:T(8,128)(2,1)} %get-tuple-element.35) | copy-start | bytes 196612
  130.1 11.2 %copy-start.44 = (bf16[64,512]{1,0:T(8,128)(2,1)S(1)}, bf16[64,512]{1,0:T(8,128)(2,1)}, u32[]{:S(2)}) copy-start(bf16[64,512]{1,0:T(8,128)(2,1)} %get-tuple-element.36) | copy-start | bytes 196612
  130.1 11.1 %copy-start.31 = (f32[128,512]{1,0:T(8,128)S(1)}, f32[128,512]{1,0:T(8,128)}, u32[]{:S(2)}) copy-start(f32[128,512]{1,0:T(8,128)} %convolution_add_fusion.3) | copy-start | bytes 786436
  131.7 18.9 %all-to-all-start.1 = ((bf16[32,4,512]{2,1,0:T(4,128)(2,1)}), bf16[32,4,512]{2,1,0:T(4,128)(2,1)S(1)}, u32[]{:S(2)}, u32[]{:S(2)}) async-start(bf16[32,4,512]{2,1,0:T(4,128)(2,1)} %reshape.209), calls=%async_computation.1 | async-start | bytes 262144 | tf_op jit(solution)/shard_map/all_to_all | solution.py:88
  134.6 276.8 %all-reduce.3.cloned.1.call-start = ((), (), s32[]{:S(2)}) async-start(), calls=%async_computation.2 | async-start | bytes 20971520 | tf_op jit(solution)/shard_map/psum | solution.py:202
  134.7 8.0 %collective-permute-start.8 = (bf16[64,512]{1,0:T(8,128)(2,1)}, bf16[64,512]{1,0:T(8,128)(2,1)S(1)}, u32[]{:S(2)}, u32[]{:S(2)}) collective-permute-start(bf16[64,512]{1,0:T(8,128)(2,1)} %get-tuple-element.33), channel_id=1, source_target_pairs={{0,7},{1,0},{2,1},{3,2},{4,3},{5,4},{6,5},{7,6},{8,15},{9,8},{10,9... | collective-permute-start | bytes 196616 | tf_op jit(solution)/shard_map/ppermute | solution.py:12
  139.5 3.9 collective-permute-start.11
  139.5 3.9 collective-permute-start.10
  141.3 12.3 %copy-start.51 = (s32[1024]{0:T(1024)S(1)}, s32[1024]{0:T(1024)}, u32[]{:S(2)}) copy-start(s32[1024]{0:T(1024)} %get-tuple-element.59) | copy-start | bytes 12292
  141.3 7.0 %collective-permute-start.9 = (bf16[64,512]{1,0:T(8,128)(2,1)S(1)}, bf16[64,512]{1,0:T(8,128)(2,1)S(1)}, u32[]{:S(2)}, u32[]{:S(2)}) collective-permute-start(bf16[64,512]{1,0:T(8,128)(2,1)S(1)} %copy-done.44), channel_id=1, source_target_pairs={{0,1},{1,2},{2,3},{3,4},{4,5},{5,6},{6,7},{7,0},{8,9},{9,10},{10,1... | collective-permute-start | bytes 196616 | tf_op jit(solution)/shard_map/ppermute | solution.py:12
  158.5 3.1 copy-start.3
  158.5 3.1 copy-start.47
  158.5 3.1 copy-start.59
  182.6 6.8 %copy-start.28 = (bf16[1024,512]{1,0:T(8,128)(2,1)S(1)}, bf16[1024,512]{1,0:T(8,128)(2,1)}, u32[]{:S(2)}) copy-start(bf16[1024,512]{1,0:T(8,128)(2,1)} %copy-done.27) | copy-start | bytes 3145732
  182.6 6.8 %copy-start.30 = (bf16[1024,512]{0,1:T(8,128)(2,1)S(1)}, bf16[1024,512]{0,1:T(8,128)(2,1)}, u32[]{:S(2)}) copy-start(bf16[1024,512]{0,1:T(8,128)(2,1)} %copy-done.29) | copy-start | bytes 3145732
  182.7 12.7 %collective-permute-start.12 = (bf16[256,512]{1,0:T(8,128)(2,1)S(1)}, bf16[256,512]{1,0:T(8,128)(2,1)S(1)}, u32[]{:S(2)}, u32[]{:S(2)}) collective-permute-start(bf16[256,512]{1,0:T(8,128)(2,1)S(1)} %get-tuple-element.25), channel_id=1, source_target_pairs={{0,7},{1,0},{2,1},{3,2},{4,3},{5,4},{6,5},{7,6},{8,15},{9,8},{10,9... | collective-permute-start | bytes 786440 | tf_op jit(solution)/shard_map/ppermute | solution.py:12
  182.8 12.6 %collective-permute-start.15 = (bf16[256,512]{1,0:T(8,128)(2,1)S(1)}, bf16[256,512]{1,0:T(8,128)(2,1)S(1)}, u32[]{:S(2)}, u32[]{:S(2)}) collective-permute-start(bf16[256,512]{1,0:T(8,128)(2,1)S(1)} %get-tuple-element.26), channel_id=1, source_target_pairs={{0,8},{8,16},{16,24},{24,0},{1,9},{9,17},{17,25},{25,1},{2,10},{10... | collective-permute-start | bytes 786440 | tf_op jit(solution)/shard_map/ppermute | solution.py:12
  182.9 12.6 %collective-permute-start.14 = (bf16[256,512]{1,0:T(8,128)(2,1)S(1)}, bf16[256,512]{1,0:T(8,128)(2,1)S(1)}, u32[]{:S(2)}, u32[]{:S(2)}) collective-permute-start(bf16[256,512]{1,0:T(8,128)(2,1)S(1)} %get-tuple-element.27), channel_id=1, source_target_pairs={{0,24},{8,0},{16,8},{24,16},{1,25},{9,1},{17,9},{25,17},{2,26},{10... | collective-permute-start | bytes 786440 | tf_op jit(solution)/shard_map/ppermute | solution.py:12
  184.6 12.3 %collective-permute-start.13 = (bf16[256,512]{1,0:T(8,128)(2,1)S(1)}, bf16[256,512]{1,0:T(8,128)(2,1)}, u32[]{:S(2)}, u32[]{:S(2)}) collective-permute-start(bf16[256,512]{1,0:T(8,128)(2,1)S(1)} %get-tuple-element.28), channel_id=1, source_target_pairs={{0,1},{1,2},{2,3},{3,4},{4,5},{5,6},{6,7},{7,0},{8,9},{9,10},{10,1... | collective-permute-start | bytes 786440 | tf_op jit(solution)/shard_map/ppermute | solution.py:12
  188.1 3.0 copy-start.16
  189.4 3.1 copy-start.21
  191.1 2.8 copy-start.39
  191.2 5.7 %slice-start = ((f32[1536,512]{1,0:T(8,128)}), f32[512,512]{1,0:T(8,128)S(1)}, s32[]{:S(2)}) async-start(f32[1536,512]{1,0:T(8,128)} %scatter_custom_fusion.3), calls=%async_computation.3 | async-start | bytes 2097152 | tf_op jit(solution)/shard_map/slice | solution.py:214
  195.4 9.7 %copy-start.32 = (bf16[512,512]{1,0:T(8,128)(2,1)S(1)}, bf16[512,512]{1,0:T(8,128)(2,1)}, u32[]{:S(2)}) copy-start(bf16[512,512]{1,0:T(8,128)(2,1)} %param.18) | copy-start | bytes 1572868
  215.6 195.8 %copy-start.71 = (f32[10]{0:T(128)S(1)}, f32[10]{0:T(128)}, u32[]{:S(2)}) copy-start(f32[10]{0:T(128)} %constant.95.clone) | copy-start | bytes 124
  419.3 8.0 %copy-start.1 = (bf16[1024,512]{1,0:T(8,128)(2,1)S(1)}, bf16[1024,512]{1,0:T(8,128)(2,1)}, u32[]{:S(2)}) copy-start(bf16[1024,512]{1,0:T(8,128)(2,1)} %param.20) | copy-start | bytes 3145732
  (37 other events, 65.6 us)
Sparse Core Ops, SparseCore 0:
  208.9 202.4 all-reduce.2
where the time goes:
time: 442 us; the launch traced here: 435 us
  waiting for transfers between devices  197 us (45%)
  local copies, waits for them, and re-layouts  71.8 us (16%)
  other arithmetic  60.3 us (14%)
  matrix products  57.1 us (13%)
  starting transfers between devices  32.7 us (7%)
  between operations  15.6 us (4%)
    psum x1, waiting for transfers between devices, on_device(): process_grads = lax.psum(process_grads, ('face', 'sub'))  191 us
    unnamed x172, local copies, waits for them, and re-layouts  24.5 us
    ppermute x16, starting transfers between devices, shifted(): return lax.ppermute(value, axis, pairs)  23.6 us
    dot_general x10, matrix products, back_product(): lax.dot_general(former, latter, (((1,), (1,)), ((), ())), preferred_eleme...  21.7 us
    dot_general x10, matrix products, product(): return jnp.dot(former, latter, preferred_element_type=jnp.float32)  18.8 us
    dot_general x16, matrix products, outer_sum(): lax.dot_general(former, latter, (((0,), (0,)), ((), ())), preferred_eleme...  16.6 us
  transfers between devices with their start and end apart: 19, of which 3 were waited for; matrix products, arithmetic and copies ran while one was open for 11% of the time, Pallas kernels for 0%

commit v1 on v0

--- a/solution.py
+++ b/solution.py
@@ -50,10 +50,19 @@
     )
 
 
-def receive_sum(onehot, values):
-    upper = values.astype(jnp.bfloat16)
-    lower = (values - upper.astype(jnp.float32)).astype(jnp.bfloat16)
-    return outer_sum(onehot, upper) + outer_sum(onehot, lower)
+def select_columns(ids, count):
+    columns = lax.broadcasted_iota(jnp.int32, (ids.shape[0], count), 1)
+    return (ids[:, None] == columns).astype(jnp.bfloat16)
+
+
+def select_pair(ids, others, count, other_count):
+    columns = lax.broadcasted_iota(jnp.int32, (ids.shape[0], count + other_count), 1)
+    hit = (ids[:, None] == columns) | ((others + count)[:, None] == columns)
+    return hit.astype(jnp.bfloat16)
+
+
+def stack_grads(terms):
+    return jnp.stack([term.astype(jnp.bfloat16) for term in terms])
 
 
 def grid_neighbours(outgoing):
@@ -111,37 +120,44 @@
     halo_table = mesh_halo[0].reshape(-1)
     far_table = mesh_send[0].reshape(-1)
     halo_count = halo_table.shape[0]
-    node_ids = jnp.arange(mesh_rows, dtype=jnp.int32)
+    slot_count = mesh_rows + halo_count + far_table.shape[0]
+    grid_slot_count = grid_rows + grid_table.shape[0]
+    pick_grid = select_columns(grid_table, grid_rows)
+    pick_halo_far = select_columns(jnp.concatenate([halo_table, far_table]), mesh_rows)
+    grid_pair = select_pair(grid_slot, grid_target, grid_slot_count, mesh_rows)
+    mesh_pair = select_pair(mesh_slot, mesh_target, slot_count, mesh_rows)
+    grid_onehot = select_columns(grid_target, mesh_rows)
+    mesh_onehot = select_columns(mesh_target, mesh_rows)
+    encode_scale = 1.0 / (grid_slot.shape[0] * peer_count) ** 0.5
+    process_scale = 1.0 / (mesh_slot.shape[0] * peer_count) ** 0.5
+    update_scale = 1.0 / (mesh_rows * peer_count) ** 0.5
     grid_project = product(grid_latent, weights[0]).astype(jnp.bfloat16)
-    grid_outgoing = jnp.take(grid_project, grid_table, axis=0).reshape(4, -1, latent)
-    grid_source = jnp.concatenate([grid_project, grid_neighbours(grid_outgoing)], axis=0)
-    encode_receive = product(mesh_latent, weights[1])
-    encoder_pre = jnp.take(grid_source, grid_slot, axis=0).astype(jnp.float32) + jnp.take(
-        encode_receive, grid_target, axis=0
-    )
+    grid_outgoing = (
+        product(pick_grid, grid_project).astype(jnp.bfloat16).reshape(4, -1, latent)
+    )
+    encode_receive = product(mesh_latent, weights[1]).astype(jnp.bfloat16)
+    grid_source = jnp.concatenate(
+        [grid_project, grid_neighbours(grid_outgoing), encode_receive], axis=0
+    )
+    encoder_pre = product(grid_pair, grid_source)
     encoder_hidden = jax.nn.silu(encoder_pre).astype(jnp.bfloat16)
     encoder_linear = product(encoder_hidden, weights[2])
     encoder_message = layer_norm(encoder_linear).astype(jnp.bfloat16)
-    grid_onehot = (grid_target[:, None] == node_ids[None, :]).astype(jnp.bfloat16)
     encoder_total = outer_sum(grid_onehot, encoder_message)
     mesh_middle = (mesh_latent.astype(jnp.float32) + encoder_total).astype(jnp.bfloat16)
     sender_rows = product(mesh_middle, weights[4]).astype(jnp.bfloat16)
-    halo_outgoing = jnp.take(sender_rows, halo_table, axis=0).reshape(4, -1, latent)
-    far_outgoing = jnp.take(sender_rows, far_table, axis=0).reshape(peer_count, -1, latent)
+    outgoing = product(pick_halo_far, sender_rows).astype(jnp.bfloat16)
+    halo_outgoing = outgoing[:halo_count].reshape(4, -1, latent)
+    far_outgoing = outgoing[halo_count:].reshape(peer_count, -1, latent)
     far_incoming = move_mesh(far_outgoing).reshape(-1, latent)
+    process_receive = product(mesh_middle, weights[5]).astype(jnp.bfloat16)
     mesh_source = jnp.concatenate(
-        [sender_rows, mesh_neighbours(halo_outgoing), far_incoming], axis=0
-    )
-    process_receive = product(mesh_middle, weights[5])
-    process_pre = (
-        product(edge_latent, weights[3])
-        + jnp.take(mesh_source, mesh_slot, axis=0).astype(jnp.float32)
-        + jnp.take(process_receive, mesh_target, axis=0)
-    )
+        [sender_rows, mesh_neighbours(halo_outgoing), far_incoming, process_receive], axis=0
+    )
+    process_pre = product(edge_latent, weights[3]) + product(mesh_pair, mesh_source)
     process_hidden = jax.nn.silu(process_pre).astype(jnp.bfloat16)
     process_linear = product(process_hidden, weights[6])
     edge_update = layer_norm(process_linear).astype(jnp.bfloat16)
-    mesh_onehot = (mesh_target[:, None] == node_ids[None, :]).astype(jnp.bfloat16)
     process_round = outer_sum(mesh_onehot, edge_update).astype(jnp.bfloat16)
     update_pre = product(mesh_middle, weights[7]) + product(process_round, weights[8])
     update_hidden = jax.nn.silu(update_pre).astype(jnp.bfloat16)
@@ -155,31 +171,27 @@
     )
     grad_update_self = outer_sum(mesh_middle, cot_update)
     grad_update_message = outer_sum(process_round, cot_update)
-    cot_total = back_product(cot_update, weights[8])
+    cot_total = back_product(cot_update, weights[8]).astype(jnp.bfloat16)
     edge_cot = edge_cotangent.astype(jnp.float32)
-    cot_edge = jnp.take(cot_total, mesh_target, axis=0) + edge_cot
+    cot_edge = product(mesh_onehot, cot_total) + edge_cot
     cot_plinear = layer_norm_back(process_linear, cot_edge).astype(jnp.bfloat16)
     grad_process_output = outer_sum(process_hidden, cot_plinear)
     cot_process = back_product(cot_plinear, weights[6]) * swish_slope(process_pre)
     cot_round = cot_process.astype(jnp.bfloat16)
     grad_process_edge = outer_sum(edge_latent, cot_round)
     edge_grad = (edge_cot + back_product(cot_round, weights[3])).astype(jnp.bfloat16)
-    cot_receive = receive_sum(mesh_onehot, cot_process).astype(jnp.bfloat16)
+    cot_slot = outer_sum(mesh_pair, cot_round)
+    cot_receive = cot_slot[slot_count:].astype(jnp.bfloat16)
     grad_process_receiver = outer_sum(mesh_middle, cot_receive)
-    cot_slot = jax.ops.segment_sum(cot_process, mesh_slot, num_segments=mesh_source.shape[0])
     halo_partials = (
         cot_slot[mesh_rows : mesh_rows + halo_count].astype(jnp.bfloat16).reshape(4, -1, latent)
     )
     far_partials = (
-        cot_slot[mesh_rows + halo_count :].astype(jnp.bfloat16).reshape(peer_count, -1, latent)
-    )
-    halo_returned = mesh_returns(halo_partials).astype(jnp.float32)
-    far_returned = return_mesh(far_partials).reshape(-1, latent).astype(jnp.float32)
-    sender_total = (
-        cot_slot[:mesh_rows]
-        + jax.ops.segment_sum(halo_returned, halo_table, num_segments=mesh_rows)
-        + jax.ops.segment_sum(far_returned, far_table, num_segments=mesh_rows)
-    )
+        cot_slot[mesh_rows + halo_count : slot_count].astype(jnp.bfloat16).reshape(peer_count, -1, latent)
+    )
+    far_returned = return_mesh(far_partials).reshape(-1, latent)
+    returned = jnp.concatenate([mesh_returns(halo_partials), far_returned], axis=0)
+    sender_total = cot_slot[:mesh_rows] + outer_sum(pick_halo_far, returned)
     cot_sender = sender_total.astype(jnp.bfloat16)
     grad_process_sender = outer_sum(mesh_middle, cot_sender)
     cot_middle = (
@@ -188,7 +200,7 @@
         + back_product(cot_receive, weights[5])
         + back_product(cot_sender, weights[4])
     )
-    process_grads = jnp.stack(
+    process_grads = stack_grads(
         [
             grad_process_edge,
             grad_process_sender,
@@ -200,28 +212,23 @@
         ]
     )
     process_grads = lax.psum(process_grads, ("face", "sub"))
-    cot_message = jnp.take(cot_middle, grid_target, axis=0)
+    cot_message = product(grid_onehot, cot_middle.astype(jnp.bfloat16))
     cot_elinear = layer_norm_back(encoder_linear, cot_message).astype(jnp.bfloat16)
     grad_encode_output = outer_sum(encoder_hidden, cot_elinear)
     cot_encoder = back_product(cot_elinear, weights[2]) * swish_slope(encoder_pre)
-    cot_mesh_receive = receive_sum(grid_onehot, cot_encoder).astype(jnp.bfloat16)
+    cot_gslot = outer_sum(grid_pair, cot_encoder.astype(jnp.bfloat16))
+    cot_mesh_receive = cot_gslot[grid_slot_count:].astype(jnp.bfloat16)
     grad_encode_receiver = outer_sum(mesh_latent, cot_mesh_receive)
     mesh_grad = (cot_middle + back_product(cot_mesh_receive, weights[1])).astype(jnp.bfloat16)
-    cot_gslot = jax.ops.segment_sum(cot_encoder, grid_slot, num_segments=grid_source.shape[0])
-    grid_partials = cot_gslot[grid_rows:].astype(jnp.bfloat16).reshape(4, -1, latent)
-    grid_returned = grid_returns(grid_partials).astype(jnp.float32)
-    cot_grid = (
-        cot_gslot[:grid_rows]
-        + jax.ops.segment_sum(grid_returned, grid_table, num_segments=grid_rows)
-    ).astype(jnp.bfloat16)
+    grid_partials = cot_gslot[grid_rows:grid_slot_count].astype(jnp.bfloat16).reshape(4, -1, latent)
+    grid_returned = grid_returns(grid_partials)
+    cot_grid = (cot_gslot[:grid_rows] + outer_sum(pick_grid, grid_returned)).astype(jnp.bfloat16)
     grad_encode_sender = outer_sum(grid_latent, cot_grid)
     grid_grad = back_product(cot_grid, weights[0]).astype(jnp.bfloat16)
-    encode_grads = jnp.stack([grad_encode_sender, grad_encode_receiver, grad_encode_output])
+    encode_grads = stack_grads([grad_encode_sender, grad_encode_receiver, grad_encode_output])
+    encode_grads, process_grads = lax.optimization_barrier((encode_grads, process_grads))
     encode_grads = lax.psum(encode_grads, ("face", "sub"))
-    summed = jnp.concatenate([encode_grads, process_grads], axis=0)
-    encode_scale = 1.0 / (grid_slot.shape[0] * peer_count) ** 0.5
-    process_scale = 1.0 / (mesh_slot.shape[0] * peer_count) ** 0.5
-    update_scale = 1.0 / (mesh_rows * peer_count) ** 0.5
+    summed = jnp.concatenate([encode_grads, process_grads], axis=0).astype(jnp.float32)
     scale_column = jnp.array(
         [encode_scale] * 3 + [process_scale] * 4 + [update_scale] * 3, jnp.float32
     )

time: 442 us -> 433 us (0.980); the launches traced: 435 us -> 431 us
  waiting for transfers between devices: 197 us -> 266 us
  other arithmetic: 60.3 us -> 14.6 us
  local copies, waits for them, and re-layouts: 71.8 us -> 26.5 us
  matrix products: 57.1 us -> 75.1 us
    psum x0 -> x1, waiting for transfers between devices: none -> 129 us  [on_device(): encode_grads = lax.psum(encode_grads, ('face', 'sub'))]
    psum x1, waiting for transfers between devices: 191 us -> 109 us  [on_device(): process_grads = lax.psum(process_grads, ('face', 'sub'))]
    gather x12 -> x0, local copies, waits for them, and re-layouts: 42.2 us -> none  [the longest x2 8.07 us: on_device(): cot_edge = jnp.take(cot_total, mesh_target, axis=0) + edge_cot]
    scatter-add x5 -> x0, other arithmetic: 28.5 us -> none  [the longest x1 8.53 us: on_device(): jax.ops.segment_sum(cot_encoder, grid_slot, num_segments=grid_source.shap...]
    ppermute x16, waiting for transfers between devices: 5.59 us -> 27.7 us  [shifted(): return lax.ppermute(value, axis, pairs)]
    dot_general x10 -> x16, matrix products: 18.8 us -> 33.8 us  [product(): return jnp.dot(former, latter, preferred_element_type=jnp.float32)]
    dot_general x16, matrix products: 16.6 us -> 26 us  [outer_sum(): lax.dot_general(former, latter, (((0,), (0,)), ((), ())), preferred_eleme...]
    dot_general x10 -> x8, matrix products: 21.7 us -> 15.3 us  [back_product(): lax.dot_general(former, latter, (((1,), (1,)), ((), ())), preferred_eleme...]
  transfers between devices with their start and end apart: 19 -> 20, of which waited for: 3 -> 7; matrix products, arithmetic and copies ran while one was open for 11% -> 9% of each run, Pallas kernels for 0% -> 0%
where the time goes in v1:
time: 433 us; the launch traced here: 431 us
  waiting for transfers between devices  266 us (61%)
  matrix products  75.1 us (17%)
  starting transfers between devices  33.9 us (8%)
  local copies, waits for them, and re-layouts  26.5 us (6%)
  between operations  14.9 us (3%)
  other arithmetic  14.6 us (3%)
    psum x1, waiting for transfers between devices, on_device(): encode_grads = lax.psum(encode_grads, ('face', 'sub'))  129 us
    psum x1, waiting for transfers between devices, on_device(): process_grads = lax.psum(process_grads, ('face', 'sub'))  109 us
    dot_general x16, matrix products, product(): return jnp.dot(former, latter, preferred_element_type=jnp.float32)  33.8 us
    ppermute x16, waiting for transfers between devices, shifted(): return lax.ppermute(value, axis, pairs)  27.7 us
    ppermute x16, starting transfers between devices, shifted(): return lax.ppermute(value, axis, pairs)  26.2 us
    dot_general x16, matrix products, outer_sum(): lax.dot_general(former, latter, (((0,), (0,)), ((), ())), preferred_eleme...  26 us
    unnamed x132, local copies, waits for them, and re-layouts  20 us
    dot_general x8, matrix products, back_product(): lax.dot_general(former, latter, (((1,), (1,)), ((), ())), preferred_eleme...  15.3 us
  transfers between devices with their start and end apart: 20, of which 7 were waited for; matrix products, arithmetic and copies ran while one was open for 9% of the time, Pallas kernels for 0%

profile of v1, /device:TPU:0, one launch (start us, length us, event | category | flops | bytes accessed | tf_op | source)
XLA Modules:
  0.0 431.3 jit_solution(9846801557097275770)
XLA Ops:
  8.0 2.5 constant_dynamic-update-slice_fusion.4
  11.2 1.0 fusion.143
  12.2 2.5 collective-permute-start.3
  14.7 4.6 %collective-permute-start.1 = (bf16[256,512]{1,0:T(8,128)(2,1)}, bf16[256,512]{1,0:T(8,128)(2,1)S(1)}, u32[]{:S(2)}, u32[]{:S(2)}) collective-permute-start(bf16[256,512]{1,0:T(8,128)(2,1)} %get-tuple-element.31), channel_id=1, source_target_pairs={{0,7},{1,0},{2,1},{3,2},{4,3},{5,4},{6,5},{7,6},{8,15},{9,8},{10,9... | collective-permute-start | bytes 786440 | tf_op jit(solution)/shard_map/ppermute | solution.py:12
  19.2 3.1 fusion.81
  22.7 1.3 copy.32
  24.0 6.8 %collective-permute-done = bf16[256,512]{1,0:T(8,128)(2,1)S(1)} collective-permute-done((bf16[256,512]{1,0:T(8,128)(2,1)}, bf16[256,512]{1,0:T(8,128)(2,1)S(1)}, u32[]{:S(2)}, u32[]{:S(2)}) %collective-permute-start) | collective-permute-done | bytes 262176 | tf_op jit(solution)/shard_map/ppermute | solution.py:12
  33.7 1.9 fusion.50
  35.6 3.6 fusion.3
  39.2 2.3 fusion.146
  42.6 1.9 constant_dynamic-update-slice_fusion.10
  45.5 1.1 collective-permute-start.4
  46.6 1.3 fusion.84
  48.5 1.6 reshape.127
  50.1 5.0 %all-to-all-start = ((bf16[32,4,512]{2,1,0:T(4,128)(2,1)}), bf16[32,4,512]{2,1,0:T(4,128)(2,1)}, u32[]{:S(2)}, u32[]{:S(2)}) async-start(bf16[32,4,512]{2,1,0:T(4,128)(2,1)} %reshape.127), calls=%async_computation | async-start | bytes 262144 | tf_op jit(solution)/shard_map/all_to_all | solution.py:93
  55.1 1.5 collective-permute-start.7
  56.6 4.3 collective-permute-start.5
  60.9 1.5 constant_dynamic-update-slice_fusion.9
  62.3 1.0 collective-permute-done.5
  65.3 1.6 reshape.128
  66.9 1.6 constant_dynamic-update-slice_fusion.5
  68.4 1.9 fusion.49
  70.4 3.0 fusion.17
  73.3 2.3 fusion.147
  77.1 1.3 convolution_add_fusion.5
  78.5 1.5 fusion.148
  81.0 1.4 fusion.46
  82.4 2.1 convolution_add_fusion.4
  84.5 4.3 %fusion.141 = (f32[1024]{0:T(1024)S(1)}, f32[1024]{0:T(1024)S(1)}, f32[1024,512]{0,1:T(8,128)}) fusion(f32[1024]{0:T(1024)S(1)} %add_rsqrt_fusion, f32[1024,512]{0,1:T(8,128)} %copy-done.2, f32[1024]{0:T(1024)S(1)} %broadcast_multiply_fusion.4, bf16[1024,512]{0,1:T(8,128)(2,1)} %copy.32, bf16[128,512]{1,0:T(8,128)(2,1)S(1)} %fusion.46, ...), kind=kOutput, calls=%fused_computation.216 | convolution fusion | flops 205191168 | bytes 5918720 | tf_op jit(solution)/shard_map/dot_general | solution.py:38
  88.9 2.9 multiply_convert_fusion.4
  91.9 2.7 multiply_convert_fusion.3
  94.6 2.6 fusion.151
  97.2 1.5 fusion.30
  98.7 5.1 %collective-permute-start.8 = (bf16[64,512]{1,0:T(8,128)(2,1)S(1)}, bf16[64,512]{1,0:T(8,128)(2,1)S(1)}, u32[]{:S(2)}, u32[]{:S(2)}) collective-permute-start(bf16[64,512]{1,0:T(8,128)(2,1)S(1)} %get-tuple-element.36), channel_id=1, source_target_pairs={{0,7},{1,0},{2,1},{3,2},{4,3},{5,4},{6,5},{7,6},{8,15},{9,8},{10,9... | collective-permute-start | bytes 196616 | tf_op jit(solution)/shard_map/ppermute | solution.py:12
  103.9 1.3 convolution_add_fusion.3
  106.0 2.6 all-to-all-start.1
  108.8 1.6 collective-permute-start.10
  110.4 1.7 collective-permute-start.9
  112.1 5.6 %collective-permute-done.9 = bf16[64,512]{1,0:T(8,128)(2,1)S(1)} collective-permute-done((bf16[64,512]{1,0:T(8,128)(2,1)S(1)}, bf16[64,512]{1,0:T(8,128)(2,1)S(1)}, u32[]{:S(2)}, u32[]{:S(2)}) %collective-permute-start.9) | collective-permute-done | bytes 65568 | tf_op jit(solution)/shard_map/ppermute | solution.py:12
  117.8 1.3 fusion.47
  119.1 1.4 convolution_add_fusion.1
  120.5 1.9 fusion.140
  122.4 1.1 fusion.36
  123.6 2.0 fusion.38
  125.7 1.6 fusion.33
  127.3 1.1 fusion.40
  128.5 1.1 fusion.42
  129.6 1.3 fusion.44
  131.0 2.1 multiply_convert_fusion.2
  133.2 6.9 %fusion.152 = (bf16[1664,512]{1,0:T(8,128)(2,1)S(1)}, f32[1664,512]{1,0:T(8,128)}) fusion(f32[1024,512]{1,0:T(8,128)} %copy-done.55, bf16[1024,512]{0,1:T(8,128)(2,1)S(1)} %multiply_convert_fusion.2, bf16[10,512,512]{2,1,0:T(8,128)(2,1)} %param.26, s32[1024]{0:T(1024)S(1)} %copy-done.32, s32[1024]{0:T(1024)S(1)} %copy-done.50), kind=kOutput, calls=%fused_computation.225 | convolution fusion | flops 2292383744 | bytes 8790016 | tf_op jit(solution)/shard_map/dot_general | solution.py:42
  140.2 1.4 collective-permute-start.12
  141.6 1.7 collective-permute-start.14
  145.2 8.8 %collective-permute-done.12 = bf16[256,512]{1,0:T(8,128)(2,1)S(1)} collective-permute-done((bf16[256,512]{1,0:T(8,128)(2,1)S(1)}, bf16[256,512]{1,0:T(8,128)(2,1)S(1)}, u32[]{:S(2)}, u32[]{:S(2)}) %collective-permute-start.12) | collective-permute-done | bytes 262176 | tf_op jit(solution)/shard_map/ppermute | solution.py:12
  154.0 5.5 %collective-permute-done.13 = bf16[256,512]{1,0:T(8,128)(2,1)S(1)} collective-permute-done((bf16[256,512]{1,0:T(8,128)(2,1)S(1)}, bf16[256,512]{1,0:T(8,128)(2,1)S(1)}, u32[]{:S(2)}, u32[]{:S(2)}) %collective-permute-start.13) | collective-permute-done | bytes 262176 | tf_op jit(solution)/shard_map/ppermute | solution.py:12
  159.5 2.3 fusion.28
  162.2 1.4 pad_maximum_fusion
  163.6 109.1 %all-reduce.3.cloned.1.call-done = bf16[7,512,512]{1,2,0:T(8,128)(2,1)} async-done(((bf16[7,512,512]{1,2,0:T(8,128)(2,1)}), bf16[7,512,512]{1,2,0:T(8,128)(2,1)}) %all-reduce.3.cloned.1.call-update) | async-done | bytes 3670032 | tf_op jit(solution)/shard_map/psum | solution.py:214
  272.7 2.1 fusion.10
  274.8 1.3 copy.41
  276.1 2.1 fusion.48
  278.2 2.3 convolution_convert_fusion.1
  280.5 129.4 %all-reduce.5.cloned.1.call-done = bf16[3,512,512]{1,2,0:T(8,128)(2,1)} async-done(((bf16[3,512,512]{1,2,0:T(8,128)(2,1)}), bf16[3,512,512]{1,2,0:T(8,128)(2,1)}) %all-reduce.5.cloned.1.call-update) | async-done | bytes 1572880 | tf_op jit(solution)/shard_map/psum | solution.py:230
  409.9 6.5 %multiply_convert_fusion = bf16[10,512,512]{1,2,0:T(8,128)(2,1)} fusion(bf16[7,512,512]{1,2,0:T(8,128)(2,1)} %all-reduce.3.cloned.1.call-done, bf16[3,512,512]{1,2,0:T(8,128)(2,1)} %all-reduce.5.cloned.1.call-done, f32[10]{0:T(128)S(1)} %copy-done.45), kind=kLoop, calls=%fused_computation | loop fusion | flops 10485760 | bytes 10485800 | tf_op jit(solution)/shard_map/convert_element_type | solution.py:235
  416.4 8.0 %copy.42 = bf16[10,512,512]{2,1,0:T(8,128)(2,1)} copy(bf16[10,512,512]{1,2,0:T(8,128)(2,1)} %multiply_convert_fusion) | data formatting | bytes 10485760
  (185 shorter events, 15.4 us)
Async XLA Ops:
  7.2 12.1 %copy-start = (bf16[1024,512]{1,0:T(8,128)(2,1)S(1)}, bf16[1024,512]{1,0:T(8,128)(2,1)}, u32[]{:S(2)}) copy-start(bf16[1024,512]{1,0:T(8,128)(2,1)} %param.16) | copy-start | bytes 3145732
  8.0 3.2 copy-start.29
  10.4 8.8 %copy-start.25 = (s32[1024]{0:T(1024)S(1)}, s32[1024]{0:T(1024)}, u32[]{:S(2)}) copy-start(s32[1024]{0:T(1024)} %param.21) | copy-start | bytes 12292
  12.2 10.1 %copy-start.22 = (s32[1024]{0:T(1024)S(1)}, s32[1024]{0:T(1024)}, u32[]{:S(2)}) copy-start(s32[1024]{0:T(1024)} %param.25) | copy-start | bytes 12292
  12.2 10.1 %copy-start.38 = (s32[1,4,64]{2,1,0:T(4,128)S(1)}, s32[1,4,64]{2,1,0:T(4,128)}, u32[]{:S(2)}) copy-start(s32[1,4,64]{2,1,0:T(4,128)} %param.22) | copy-start | bytes 3076
  12.2 10.2 %copy-start.37 = (s32[1,32,4]{1,2,0:T(4,128)S(1)}, s32[1,32,4]{1,2,0:T(4,128)}, u32[]{:S(2)}) copy-start(s32[1,32,4]{1,2,0:T(4,128)} %param.23) | copy-start | bytes 1540
  12.2 10.4 %copy-start.10 = (bf16[1024,512]{1,0:T(8,128)(2,1)S(1)}, bf16[1024,512]{1,0:T(8,128)(2,1)}, u32[]{:S(2)}) copy-start(bf16[1024,512]{1,0:T(8,128)(2,1)} %param.18) | copy-start | bytes 3145732
  12.2 20.8 %collective-permute-start.3 = (bf16[256,512]{1,0:T(8,128)(2,1)}, bf16[256,512]{1,0:T(8,128)(2,1)S(1)}, u32[]{:S(2)}, u32[]{:S(2)}) collective-permute-start(bf16[256,512]{1,0:T(8,128)(2,1)} %get-tuple-element.29), channel_id=1, source_target_pairs={{0,24},{8,0},{16,8},{24,16},{1,25},{9,1},{17,9},{25,17},{2,26},{10... | collective-permute-start | bytes 786440 | tf_op jit(solution)/shard_map/ppermute | solution.py:12
  14.7 17.6 %collective-permute-start.2 = (bf16[256,512]{1,0:T(8,128)(2,1)}, bf16[256,512]{1,0:T(8,128)(2,1)S(1)}, u32[]{:S(2)}, u32[]{:S(2)}) collective-permute-start(bf16[256,512]{1,0:T(8,128)(2,1)} %get-tuple-element.30), channel_id=1, source_target_pairs={{0,8},{8,16},{16,24},{24,0},{1,9},{9,17},{17,25},{25,1},{2,10},{10... | collective-permute-start | bytes 786440 | tf_op jit(solution)/shard_map/ppermute | solution.py:12
  14.7 16.9 %collective-permute-start.1 = (bf16[256,512]{1,0:T(8,128)(2,1)}, bf16[256,512]{1,0:T(8,128)(2,1)S(1)}, u32[]{:S(2)}, u32[]{:S(2)}) collective-permute-start(bf16[256,512]{1,0:T(8,128)(2,1)} %get-tuple-element.31), channel_id=1, source_target_pairs={{0,7},{1,0},{2,1},{3,2},{4,3},{5,4},{6,5},{7,6},{8,15},{9,8},{10,9... | collective-permute-start | bytes 786440 | tf_op jit(solution)/shard_map/ppermute | solution.py:12
  19.2 11.6 %collective-permute-start = (bf16[256,512]{1,0:T(8,128)(2,1)}, bf16[256,512]{1,0:T(8,128)(2,1)S(1)}, u32[]{:S(2)}, u32[]{:S(2)}) collective-permute-start(bf16[256,512]{1,0:T(8,128)(2,1)} %get-tuple-element.32), channel_id=1, source_target_pairs={{0,1},{1,2},{2,3},{3,4},{4,5},{5,6},{6,7},{7,0},{8,9},{9,10},{10,1... | collective-permute-start | bytes 786440 | tf_op jit(solution)/shard_map/ppermute | solution.py:12
  19.2 16.4 %copy-start.31 = (s32[1024]{0:T(1024)}, s32[1024]{0:T(1024)S(1)}, u32[]{:S(2)}) copy-start(s32[1024]{0:T(1024)S(1)} %broadcast_add_fusion.1) | copy-start | bytes 12292
  22.3 48.0 %copy-start.33 = (s32[1024]{0:T(1024)}, s32[1024]{0:T(1024)S(1)}, u32[]{:S(2)}) copy-start(s32[1024]{0:T(1024)S(1)} %broadcast_add_fusion) | copy-start | bytes 12292
  22.6 21.9 %copy-start.27 = (s32[384]{0:T(512)}, s32[384]{0:T(512)S(1)}, u32[]{:S(2)}) copy-start(s32[384]{0:T(512)S(1)} %pad_add_fusion) | copy-start | bytes 4612
  22.6 11.0 %copy-start.16 = (bf16[128,512]{1,0:T(8,128)(2,1)S(1)}, bf16[128,512]{1,0:T(8,128)(2,1)}, u32[]{:S(2)}) copy-start(bf16[128,512]{1,0:T(8,128)(2,1)} %param.15) | copy-start | bytes 393220
  22.7 13.0 %copy-start.49 = (s32[1024]{0:T(1024)S(1)}, s32[1024]{0:T(1024)}, u32[]{:S(2)}) copy-start(s32[1024]{0:T(1024)} %param.20) | copy-start | bytes 12292
  44.8 25.5 %copy-start.47 = (s32[1024]{0:T(1024)S(1)}, s32[1024]{0:T(1024)}, u32[]{:S(2)}) copy-start(s32[1024]{0:T(1024)} %param.24) | copy-start | bytes 12292
  45.5 15.3 %collective-permute-start.4 = (bf16[64,512]{1,0:T(8,128)(2,1)}, bf16[64,512]{1,0:T(8,128)(2,1)}, u32[]{:S(2)}, u32[]{:S(2)}) collective-permute-start(bf16[64,512]{1,0:T(8,128)(2,1)} %get-tuple-element.40), channel_id=1, source_target_pairs={{0,1},{1,2},{2,3},{3,4},{4,5},{5,6},{6,7},{7,0},{8,9},{9,10},{10,1... | collective-permute-start | bytes 196616 | tf_op jit(solution)/shard_map/ppermute | solution.py:12
  50.1 15.1 %all-to-all-start = ((bf16[32,4,512]{2,1,0:T(4,128)(2,1)}), bf16[32,4,512]{2,1,0:T(4,128)(2,1)}, u32[]{:S(2)}, u32[]{:S(2)}) async-start(bf16[32,4,512]{2,1,0:T(4,128)(2,1)} %reshape.127), calls=%async_computation | async-start | bytes 262144 | tf_op jit(solution)/shard_map/all_to_all | solution.py:93
  55.1 9.5 %collective-permute-start.7 = (bf16[64,512]{1,0:T(8,128)(2,1)}, bf16[64,512]{1,0:T(8,128)(2,1)S(1)}, u32[]{:S(2)}, u32[]{:S(2)}) collective-permute-start(bf16[64,512]{1,0:T(8,128)(2,1)} %get-tuple-element.37), channel_id=1, source_target_pairs={{0,24},{8,0},{16,8},{24,16},{1,25},{9,1},{17,9},{25,17},{2,26},{10... | collective-permute-start | bytes 196616 | tf_op jit(solution)/shard_map/ppermute | solution.py:12
  56.6 7.4 %collective-permute-start.6 = (bf16[64,512]{1,0:T(8,128)(2,1)}, bf16[64,512]{1,0:T(8,128)(2,1)S(1)}, u32[]{:S(2)}, u32[]{:S(2)}) collective-permute-start(bf16[64,512]{1,0:T(8,128)(2,1)} %get-tuple-element.38), channel_id=1, source_target_pairs={{0,8},{8,16},{16,24},{24,0},{1,9},{9,17},{17,25},{25,1},{2,10},{10... | collective-permute-start | bytes 196616 | tf_op jit(solution)/shard_map/ppermute | solution.py:12
  56.6 6.8 %collective-permute-start.5 = (bf16[64,512]{1,0:T(8,128)(2,1)}, bf16[64,512]{1,0:T(8,128)(2,1)S(1)}, u32[]{:S(2)}, u32[]{:S(2)}) collective-permute-start(bf16[64,512]{1,0:T(8,128)(2,1)} %get-tuple-element.39), channel_id=1, source_target_pairs={{0,7},{1,0},{2,1},{3,2},{4,3},{5,4},{6,5},{7,6},{8,15},{9,8},{10,9... | collective-permute-start | bytes 196616 | tf_op jit(solution)/shard_map/ppermute | solution.py:12
  77.1 5.3 %copy-start.6 = (bf16[128,512]{1,0:T(8,128)(2,1)}, bf16[128,512]{1,0:T(8,128)(2,1)S(1)}, u32[]{:S(2)}) copy-start(bf16[128,512]{1,0:T(8,128)(2,1)S(1)} %convolution_convert_fusion.17) | copy-start | bytes 393220
  77.1 3.1 copy-start.18
  78.5 3.9 copy-start.20
  80.2 4.3 %copy-start.39 = (f32[128]{0:T(128)}, f32[128]{0:T(128)S(1)}, u32[]{:S(2)}) copy-start(f32[128]{0:T(128)S(1)} %add_rsqrt_fusion.2) | copy-start | bytes 1540
  80.2 4.3 %copy-start.24 = (s32[1024]{0:T(1024)S(1)}, s32[1024]{0:T(1024)}, u32[]{:S(2)}) copy-start(s32[1024]{0:T(1024)} %param.25) | copy-start | bytes 12292
  81.0 7.9 %copy-start.41 = (f32[128]{0:T(128)}, f32[128]{0:T(128)S(1)}, u32[]{:S(2)}) copy-start(f32[128]{0:T(128)S(1)} %get-tuple-element.58) | copy-start | bytes 1540
  81.0 7.9 %copy-start.43 = (f32[128]{0:T(128)}, f32[128]{0:T(128)S(1)}, u32[]{:S(2)}) copy-start(f32[128]{0:T(128)S(1)} %get-tuple-element.59) | copy-start | bytes 1540
  82.4 6.5 %copy-start.4 = (bf16[128,512]{1,0:T(8,128)(2,1)}, bf16[128,512]{1,0:T(8,128)(2,1)S(1)}, u32[]{:S(2)}) copy-start(bf16[128,512]{1,0:T(8,128)(2,1)S(1)} %fusion.46) | copy-start | bytes 393220
  88.9 2.9 copy-start.52
  91.9 2.7 copy-start.8
  91.9 2.7 copy-start.34
  97.2 8.1 %copy-start.15 = (bf16[640,512]{1,0:T(8,128)(2,1)}, bf16[640,512]{1,0:T(8,128)(2,1)S(1)}, u32[]{:S(2)}) copy-start(bf16[640,512]{1,0:T(8,128)(2,1)S(1)} %get-tuple-element.53) | copy-start | bytes 1966084
  97.2 6.7 %copy-start.13 = (f32[128,512]{1,0:T(8,128)S(1)}, f32[128,512]{1,0:T(8,128)}, u32[]{:S(2)}) copy-start(f32[128,512]{1,0:T(8,128)} %convolution_add_fusion.4) | copy-start | bytes 786436
  98.7 19.1 %copy-start.28 = (s32[384]{0:T(512)S(1)}, s32[384]{0:T(512)}, u32[]{:S(2)}) copy-start(s32[384]{0:T(512)} %copy-done.27) | copy-start | bytes 4612
  98.7 13.3 %collective-permute-start.8 = (bf16[64,512]{1,0:T(8,128)(2,1)S(1)}, bf16[64,512]{1,0:T(8,128)(2,1)S(1)}, u32[]{:S(2)}, u32[]{:S(2)}) collective-permute-start(bf16[64,512]{1,0:T(8,128)(2,1)S(1)} %get-tuple-element.36), channel_id=1, source_target_pairs={{0,7},{1,0},{2,1},{3,2},{4,3},{5,4},{6,5},{7,6},{8,15},{9,8},{10,9... | collective-permute-start | bytes 196616 | tf_op jit(solution)/shard_map/ppermute | solution.py:12
  105.2 15.2 %copy-start.26 = (s32[1024]{0:T(1024)S(1)}, s32[1024]{0:T(1024)}, u32[]{:S(2)}) copy-start(s32[1024]{0:T(1024)} %param.21) | copy-start | bytes 12292
  106.0 11.8 %all-to-all-start.1 = ((bf16[32,4,512]{2,1,0:T(4,128)(2,1)}), bf16[32,4,512]{2,1,0:T(4,128)(2,1)S(1)}, u32[]{:S(2)}, u32[]{:S(2)}) async-start(bf16[32,4,512]{2,1,0:T(4,128)(2,1)} %reshape.129), calls=%async_computation.1 | async-start | bytes 262144 | tf_op jit(solution)/shard_map/all_to_all | solution.py:97
  108.5 164.1 %all-reduce.3.cloned.1.call-start = ((), (), s32[]{:S(2)}) async-start(), calls=%async_computation.2 | async-start | bytes 7340032 | tf_op jit(solution)/shard_map/psum | solution.py:214
  108.6 9.1 %collective-permute-start.11 = (bf16[64,512]{1,0:T(8,128)(2,1)S(1)}, bf16[64,512]{1,0:T(8,128)(2,1)S(1)}, u32[]{:S(2)}, u32[]{:S(2)}) collective-permute-start(bf16[64,512]{1,0:T(8,128)(2,1)S(1)} %get-tuple-element.33), channel_id=1, source_target_pairs={{0,8},{8,16},{16,24},{24,0},{1,9},{9,17},{17,25},{25,1},{2,10},{10... | collective-permute-start | bytes 196616 | tf_op jit(solution)/shard_map/ppermute | solution.py:12
  108.8 8.9 %collective-permute-start.10 = (bf16[64,512]{1,0:T(8,128)(2,1)S(1)}, bf16[64,512]{1,0:T(8,128)(2,1)S(1)}, u32[]{:S(2)}, u32[]{:S(2)}) collective-permute-start(bf16[64,512]{1,0:T(8,128)(2,1)S(1)} %get-tuple-element.34), channel_id=1, source_target_pairs={{0,24},{8,0},{16,8},{24,16},{1,25},{9,1},{17,9},{25,17},{2,26},{10... | collective-permute-start | bytes 196616 | tf_op jit(solution)/shard_map/ppermute | solution.py:12
  110.4 7.3 %collective-permute-start.9 = (bf16[64,512]{1,0:T(8,128)(2,1)S(1)}, bf16[64,512]{1,0:T(8,128)(2,1)S(1)}, u32[]{:S(2)}, u32[]{:S(2)}) collective-permute-start(bf16[64,512]{1,0:T(8,128)(2,1)S(1)} %get-tuple-element.35), channel_id=1, source_target_pairs={{0,1},{1,2},{2,3},{3,4},{4,5},{5,6},{6,7},{7,0},{8,9},{9,10},{10,1... | collective-permute-start | bytes 196616 | tf_op jit(solution)/shard_map/ppermute | solution.py:12
  120.5 5.1 %copy-start.9 = (bf16[1024,512]{0,1:T(8,128)(2,1)S(1)}, bf16[1024,512]{0,1:T(8,128)(2,1)}, u32[]{:S(2)}) copy-start(bf16[1024,512]{0,1:T(8,128)(2,1)} %copy-done.8) | copy-start | bytes 3145732
  120.5 5.1 %copy-start.53 = (f32[1024,512]{1,0:T(8,128)S(1)}, f32[1024,512]{1,0:T(8,128)}, u32[]{:S(2)}) copy-start(f32[1024,512]{1,0:T(8,128)} %copy-done.51) | copy-start | bytes 6291460
  125.6 2.8 copy-start.7
  125.6 4.0 copy-start.12
  125.6 4.0 copy-start.19
  125.7 4.0 copy-start.21
  125.7 4.0 copy-start.36
  125.7 3.9 copy-start.40
  125.7 3.9 copy-start.42
  125.7 3.9 copy-start.44
  130.9 279.0 %all-reduce.5.cloned.1.call-start = ((), (), s32[]{:S(2)}) async-start(), calls=%async_computation.3 | async-start | bytes 3145728 | tf_op jit(solution)/shard_map/psum | solution.py:230
  140.1 4.7 %copy-start.14 = (bf16[1664,512]{1,0:T(8,128)(2,1)}, bf16[1664,512]{1,0:T(8,128)(2,1)S(1)}, u32[]{:S(2)}) copy-start(bf16[1664,512]{1,0:T(8,128)(2,1)S(1)} %get-tuple-element.56) | copy-start | bytes 5111812
  140.1 3.9 copy-start.56
  140.2 13.8 %collective-permute-start.12 = (bf16[256,512]{1,0:T(8,128)(2,1)S(1)}, bf16[256,512]{1,0:T(8,128)(2,1)S(1)}, u32[]{:S(2)}, u32[]{:S(2)}) collective-permute-start(bf16[256,512]{1,0:T(8,128)(2,1)S(1)} %get-tuple-element.25), channel_id=1, source_target_pairs={{0,7},{1,0},{2,1},{3,2},{4,3},{5,4},{6,5},{7,6},{8,15},{9,8},{10,9... | collective-permute-start | bytes 786440 | tf_op jit(solution)/shard_map/ppermute | solution.py:12
  141.6 12.4 %collective-permute-start.15 = (bf16[256,512]{1,0:T(8,128)(2,1)S(1)}, bf16[256,512]{1,0:T(8,128)(2,1)S(1)}, u32[]{:S(2)}, u32[]{:S(2)}) collective-permute-start(bf16[256,512]{1,0:T(8,128)(2,1)S(1)} %get-tuple-element.26), channel_id=1, source_target_pairs={{0,8},{8,16},{16,24},{24,0},{1,9},{9,17},{17,25},{25,1},{2,10},{10... | collective-permute-start | bytes 786440 | tf_op jit(solution)/shard_map/ppermute | solution.py:12
  141.6 12.4 %collective-permute-start.14 = (bf16[256,512]{1,0:T(8,128)(2,1)S(1)}, bf16[256,512]{1,0:T(8,128)(2,1)S(1)}, u32[]{:S(2)}, u32[]{:S(2)}) collective-permute-start(bf16[256,512]{1,0:T(8,128)(2,1)S(1)} %get-tuple-element.27), channel_id=1, source_target_pairs={{0,24},{8,0},{16,8},{24,16},{1,25},{9,1},{17,9},{25,17},{2,26},{10... | collective-permute-start | bytes 786440 | tf_op jit(solution)/shard_map/ppermute | solution.py:12
  143.4 16.1 %copy-start.30 = (s32[1,2,4,128]{3,1,2,0:T(2,128)S(1)}, s32[1,2,4,128]{3,1,2,0:T(2,128)}, u32[]{:S(2)}) copy-start(s32[1,2,4,128]{3,1,2,0:T(2,128)} %copy-done.29) | copy-start | bytes 12292
  143.4 16.1 %collective-permute-start.13 = (bf16[256,512]{1,0:T(8,128)(2,1)S(1)}, bf16[256,512]{1,0:T(8,128)(2,1)S(1)}, u32[]{:S(2)}, u32[]{:S(2)}) collective-permute-start(bf16[256,512]{1,0:T(8,128)(2,1)S(1)} %get-tuple-element.28), channel_id=1, source_target_pairs={{0,1},{1,2},{2,3},{3,4},{4,5},{5,6},{6,7},{7,0},{8,9},{9,10},{10,1... | collective-permute-start | bytes 786440 | tf_op jit(solution)/shard_map/ppermute | solution.py:12
  162.2 110.5 %copy-start.3 = (bf16[1024,512]{0,1:T(8,128)(2,1)S(1)}, bf16[1024,512]{0,1:T(8,128)(2,1)}, u32[]{:S(2)}) copy-start(bf16[1024,512]{0,1:T(8,128)(2,1)} %copy.32) | copy-start | bytes 3145732
  274.8 135.1 %copy-start.45 = (f32[10]{0:T(128)S(1)}, f32[10]{0:T(128)}, u32[]{:S(2)}) copy-start(f32[10]{0:T(128)} %constant.34.clone) | copy-start | bytes 124
  416.4 8.0 %copy-start.1 = (bf16[1024,512]{1,0:T(8,128)(2,1)S(1)}, bf16[1024,512]{1,0:T(8,128)(2,1)}, u32[]{:S(2)}) copy-start(bf16[1024,512]{1,0:T(8,128)(2,1)} %param.16) | copy-start | bytes 3145732
  (13 other events, 25.4 us)
Sparse Core Ops, SparseCore 0:
  131.1 141.5 all-reduce.2
  278.0 131.9 all-reduce.4
